TPU v7x, 32 devices: a whole 2x2x4 slice. The times are simulated.
32 devices in a mesh: rep: 4 (over y, x), col: 8 (over z, core).
Axes of the slice: x: 2, y: 2, z: 4, core: 2. Of those that a mesh axis runs over, the one named last changes fastest.
Arguments:
- tables: float32 [2, 256, 32768], P(None, 'col', 'rep'), may hold values from -4 to 4
- accumulator: float32 [2, 32768], P(None, 'rep'), may hold values from 0.1 to 20
- replica_grads: bfloat16 [4, 2, 256, 16384], P('rep', None, 'col'), may hold values from -6 to 6
- block_ids: int32 [2, 128], replicated, may hold values from 0 to 255, as said below
Outputs:
- new_tables: float32 [2, 256, 32768], P(None, 'col', 'rep')
- new_accumulator: float32 [2, 32768], P(None, 'rep')
Inputs may be any that keep to these rules, and one draw needn't show every extreme that they name: `block_ids`: the block ids of one table are distinct; each names a block of 128 rows. Splitting the 32768 rows into 4 equal runs, each run holds exactly 32 of a table's touched blocks.
All inputs are finite; a program needn't handle non-finite values.
Results may differ from a plain program's by a relative error of at most 0.0003.
Values sent between devices are 32-bit elements; how exact they have to be, the bound alone decides.
A program may use at most 64 MiB of HBM per device.

v0:
```python
import jax
import jax.numpy as jnp
from jax import lax
from jax.sharding import PartitionSpec as P

DIM = 256
BLOCK = 128


def row_squares(total):
    return lax.psum(jnp.sum(total * total, axis=1), "col")


def body(tables, accumulator, replica_grads, block_ids):
    own_grad = replica_grads[0].astype(jnp.float32)
    ntab, width, local_rows = tables.shape
    local_blocks = local_rows // BLOCK
    offset = lax.axis_index("rep") * local_blocks
    full_blocks = own_grad.shape[2] // BLOCK
    per_owner = full_blocks // lax.axis_size("rep")
    arranged = []
    owned_ids = []
    for table in range(ntab):
        owner = block_ids[table] // local_blocks
        order = jnp.argsort(owner, stable=True)
        grouped = own_grad[table].reshape(width, full_blocks, BLOCK)
        arranged.append(jnp.take(grouped, order, axis=1).reshape(width, full_blocks * BLOCK))
        sorted_ids = jnp.take(block_ids[table], order, axis=0)
        owned_ids.append(
            lax.dynamic_slice_in_dim(sorted_ids, lax.axis_index("rep") * per_owner, per_owner)
        )
    total = lax.psum_scatter(jnp.stack(arranged), "rep", scatter_dimension=2, tiled=True)
    squares = row_squares(total)
    used_ids = jnp.stack(owned_ids)
    slab = total.shape[2]
    nblk = slab // BLOCK
    blocked = tables.reshape(ntab, width, local_blocks, BLOCK)
    acc_blocked = accumulator.reshape(ntab, local_blocks, BLOCK)
    out_tab = []
    out_acc = []
    for table in range(ntab):
        local_ids = used_ids[table] - offset
        inside = (local_ids >= 0) & (local_ids < local_blocks)
        safe_ids = jnp.where(inside, local_ids, 0)
        target = jnp.where(inside, local_ids, local_blocks)
        old_rows = jnp.take(blocked[table], safe_ids, axis=1).reshape(width, slab)
        old_accum = jnp.take(acc_blocked[table], safe_ids, axis=0).reshape(slab)
        fresh = old_accum + squares[table] / DIM
        moved = old_rows - 0.1 * total[table] / (jnp.sqrt(fresh)[None, :] + 1e-08)
        new_blocks = (
            blocked[table].at[:, target].set(moved.reshape(width, nblk, BLOCK), mode="drop")
        )
        new_acc = acc_blocked[table].at[target].set(fresh.reshape(nblk, BLOCK), mode="drop")
        out_tab.append(new_blocks.reshape(width, local_rows))
        out_acc.append(new_acc.reshape(local_rows))
    return (jnp.stack(out_tab), jnp.stack(out_acc))


def solution(mesh):
    return jax.shard_map(
        body,
        mesh=mesh,
        in_specs=(P(None, "col", "rep"), P(None, "rep"), P("rep", None, "col", None), P()),
        out_specs=(P(None, "col", "rep"), P(None, "rep")),
        check_vma=False,
    )
```

profile of v0, /device:TPU:0, one launch (start us, length us, event | category | flops | bytes accessed | tf_op | source)
XLA Modules:
  0.0 150.6 jit_solution(7778629519587096425)
XLA Ops:
  7.2 0.8 and_select_fusion.1
  8.0 0.8 slice_bitcast_fusion.5
  8.7 2.5 %sort.31 = (s32[128]{0:T(128)}, s32[128]{0:T(128)S(1)}) sort(s32[128]{0:T(128)S(1)} %get-tuple-element.32, s32[128]{0:T(128)S(1)} %iota.7), dimensions={0}, to_apply=%region_0.1 | sort | flops 896 | bytes 2048 | tf_op jit(solution)/shard_map/jit(argsort)/sort | solution.py:25
  11.3 1.2 gather_fusion
  12.5 2.5 %sort.32 = (s32[128]{0:T(128)}, s32[128]{0:T(128)S(1)}) sort(s32[128]{0:T(128)S(1)} %get-tuple-element.33, s32[128]{0:T(128)S(1)} %iota.8), dimensions={0}, to_apply=%region_1.0 | sort | flops 896 | bytes 2048 | tf_op jit(solution)/shard_map/jit(argsort)/sort | solution.py:25
  15.1 1.2 gather_fusion.5
  16.3 1.9 %convert_element_type.4 = f32[1,2,32,16384]{3,2,1,0:T(8,128)S(1)} convert(bf16[1,2,32,16384]{3,2,1,0:T(8,128)(2,1)} %param.14) | non-fusion elementwise | flops 1048576 | bytes 6291456 | tf_op jit(solution)/shard_map/convert_element_type | solution.py:15
  18.2 1.6 %slice_bitcast_fusion.1 = (f32[4,8,128,128]{3,1,2,0:T(8,128)S(1)}, f32[4,8,128,128]{3,1,2,0:T(8,128)}) fusion(f32[1,2,32,16384]{3,2,1,0:T(8,128)S(1)} %convert_element_type.4), kind=kLoop, calls=%fused_computation.14 | loop fusion | bytes 8388608
  20.2 2.6 %copy.13 = f32[32,128,128]{2,0,1:T(8,128)} copy(f32[32,128,128]{2,1,0:T(8,128)S(1)} %bitcast.60) | data formatting | bytes 4194304 | tf_op jit(solution)/shard_map/reshape;squeeze | solution.py:26
  22.8 2.3 %gather_fusion.2 = f32[128,32,128]{2,1,0:T(8,128)S(1)} fusion(f32[32,128,128]{2,0,1:T(8,128)} %copy.13, s32[1024]{0:T(1024)S(1)} %pad_clamp_fusion.3), kind=kCustom, calls=%fused_computation.2.clone | custom fusion | bytes 4194816 | tf_op jit(solution)/shard_map/jit(_take)/gather | solution.py:27
  25.3 1.2 copy.14
  26.5 1.5 %stack_reshape.18 = f32[1,32,16384]{2,1,0:T(8,128)} reshape(f32[32,128,128]{2,1,0:T(8,128)S(1)} %copy.14) | data formatting | bytes 4194304 | tf_op jit(solution)/shard_map/stack;reshape | solution.py:32
  28.0 2.0 %copy.26 = f32[4,8,128,128]{3,2,1,0:T(8,128)S(1)} copy(f32[4,8,128,128]{3,1,2,0:T(8,128)} %get-tuple-element.19) | data formatting | bytes 4194304
  30.0 2.5 %copy.15 = f32[32,128,128]{2,0,1:T(8,128)} copy(f32[32,128,128]{2,1,0:T(8,128)S(1)} %bitcast.61) | data formatting | bytes 4194304 | tf_op jit(solution)/shard_map/reshape;squeeze | solution.py:26
  32.5 2.3 %gather_fusion.3 = f32[128,32,128]{2,1,0:T(8,128)S(1)} fusion(f32[32,128,128]{2,0,1:T(8,128)} %copy.15, s32[1024]{0:T(1024)S(1)} %pad_clamp_fusion.1), kind=kCustom, calls=%fused_computation.6.clone | custom fusion | bytes 4194816 | tf_op jit(solution)/shard_map/jit(_take)/gather | solution.py:27
  35.0 1.2 copy.16
  36.3 1.5 %stack_reshape.19 = f32[1,32,16384]{2,1,0:T(8,128)} reshape(f32[32,128,128]{2,1,0:T(8,128)S(1)} %copy.16) | data formatting | bytes 4194304 | tf_op jit(solution)/shard_map/stack;reshape | solution.py:32
  37.8 4.4 %pad_maximum_fusion = f32[2,32,16384]{2,1,0:T(8,128)} fusion(f32[1,32,16384]{2,1,0:T(8,128)} %stack_reshape.19, f32[1,32,16384]{2,1,0:T(8,128)} %stack_reshape.18), kind=kLoop, calls=%fused_computation.12 | loop fusion | flops 1048576 | bytes 8388608 | tf_op jit(solution)/shard_map/stack | solution.py:32
  42.3 1.7 %slice_bitcast_fusion.3 = (f32[4,8,64,128]{3,1,2,0:T(8,128)S(1)}, f32[4,8,64,128]{3,1,2,0:T(8,128)S(1)}) fusion(f32[2,32,8192]{2,1,0:T(8,128)} %param.12), kind=kLoop, calls=%fused_computation.20 | loop fusion | bytes 4194304
  47.5 1.4 gather_fusion.6
  49.2 48.6 %reduce-scatter.2.cloned.1.call-done = f32[2,32,4096]{2,1,0:T(8,128)} async-done(((f32[2,32,16384]{2,1,0:T(8,128)}), f32[2,32,4096]{2,1,0:T(8,128)}) %reduce-scatter.2.cloned.1.call-update) | async-done | bytes 1048592 | tf_op jit(solution)/shard_map/reduce_scatter | solution.py:32
  97.7 1.4 multiply_reduce_fusion
  99.1 28.4 %psum.7 = f32[2,4096]{1,0:T(2,128)S(1)} all-reduce(f32[2,4096]{1,0:T(2,128)S(1)} %multiply_reduce_fusion), channel_id=1, replica_groups=mesh['rep'=4,'col'=8] {'col'}, use_global_device_ids=true, to_apply=%region_4.9 | all-reduce | flops 8192 | bytes 65536 | tf_op jit(solution)/shard_map/psum | solution.py:11
  127.5 2.1 %fusion.1 = (f32[4,8,32,128]{3,1,2,0:T(8,128)S(1)}, f32[4,8,32,128]{3,1,2,0:T(8,128)}) fusion(f32[2,32,4096]{2,1,0:T(8,128)} %reduce-scatter.2.cloned.1.call-done), kind=kLoop, calls=%fused_computation.24 | loop fusion | flops 262144 | bytes 2097152
  129.8 0.8 scatter_custom_fusion.2
  130.6 1.1 fusion.3
  131.8 3.4 %scatter_fusion = f32[32,64,128]{2,0,1:T(8,128)S(1)} fusion(f32[32,64,128]{2,0,1:T(8,128)S(1)} %copy.18, s32[32]{0:T(128)S(1)} %get-tuple-element.35, f32[32,32,128]{2,1,0:T(8,128)} %fusion.3), kind=kCustom, calls=%fused_computation.8 | custom fusion | bytes 1572992 | tf_op jit(solution)/shard_map/scatter | solution.py:51
  135.7 1.2 stack_reshape.20
  136.9 1.1 copy.29
  138.0 0.8 scatter_custom_fusion.3
  139.2 1.5 %scatter_fusion.1 = f32[32,64,128]{2,0,1:T(8,128)S(1)} fusion(f32[32,64,128]{2,0,1:T(8,128)S(1)} %copy.22, s32[32]{0:T(128)S(1)} %get-tuple-element.34, f32[32,32,128]{2,1,0:T(8,128)S(1)} %fusion.2), kind=kCustom, calls=%fused_computation.9 | custom fusion | bytes 1572992 | tf_op jit(solution)/shard_map/scatter | solution.py:51
  142.3 1.5 pad_maximum_fusion.1
  (40 shorter events, 7.3 us)
Async XLA Ops:
  7.2 90.6 %reduce-scatter.2.cloned.1.call-start = ((), (), s32[]{:S(2)}) async-start(), calls=%async_computation.1 | async-start | bytes 5242880 | tf_op jit(solution)/shard_map/reduce_scatter | solution.py:32
  44.0 0.9 copy-start.2
  135.7 3.1 %copy-start.1 = (f32[32,32,128]{2,1,0:T(8,128)S(1)}, f32[32,32,128]{2,1,0:T(8,128)}, u32[]{:S(2)}) copy-start(f32[32,32,128]{2,1,0:T(8,128)} %gather_fusion.6) | copy-start | bytes 1572868
  140.7 1.5 %copy-start = (f32[1,32,8192]{2,1,0:T(8,128)S(1)}, f32[1,32,8192]{2,1,0:T(8,128)}, u32[]{:S(2)}) copy-start(f32[1,32,8192]{2,1,0:T(8,128)} %stack_reshape.20) | copy-start | bytes 3145732
Sparse Core Ops, SparseCore 0:
  42.4 55.3 reduce-scatter.1
where the time goes:
time: 151 us
  waiting for transfers between devices  48.6 us (32%)
  local copies, waits for them, and re-layouts  37.5 us (25%)
  blocking collectives  28.4 us (19%)
  other arithmetic  21.7 us (14%)
  between operations  14.3 us (9%)
    reduce_scatter x1, waiting for transfers between devices, body(): lax.psum_scatter(jnp.stack(arranged), 'rep', scatter_dimension=2, tiled=T...  48.6 us
    psum x1, blocking collectives, row_squares(): return lax.psum(jnp.sum(total * total, axis=1), 'col')  28.4 us
    unnamed x14, local copies, waits for them, and re-layouts  7.26 us
    scatter x4, local copies, waits for them, and re-layouts, body(): blocked[table].at[:, target]  6.1 us
    another operation x2, local copies, waits for them, and re-layouts, body(): grouped = own_grad[table].reshape(width, full_blocks, BLOCK)  5.11 us
    sort x2, other arithmetic, body(): order = jnp.argsort(owner, stable=True)  5.07 us
    gather x2, local copies, waits for them, and re-layouts, body(): jnp.take(grouped, order, axis=1).reshape(width, full_blocks * BLOCK)  4.54 us
    another operation x1, other arithmetic, body(): jnp.stack(arranged)  4.45 us
  transfers between devices with their start and end apart: 1, of which 1 were waited for; matrix products, arithmetic and copies ran while one was open for 5% of the time, Pallas kernels for 0%

commit v1 on v0

--- a/solution.py
+++ b/solution.py
@@ -7,8 +7,14 @@
 BLOCK = 128
 
 
+def summed_here(x, axis):
+    parts = lax.all_gather(x, axis, axis=0, tiled=False)
+    total = parts.sum(axis=0)
+    return total
+
+
 def row_squares(total):
-    return lax.psum(jnp.sum(total * total, axis=1), "col")
+    return summed_here(jnp.sum(total * total, axis=1), "col")
 
 
 def body(tables, accumulator, replica_grads, block_ids):

time: 151 us -> 138 us (0.914)
  blocking collectives: 28.4 us -> 14.4 us
  other arithmetic: 21.7 us -> 23.3 us
    psum x1 -> x0, blocking collectives: 28.4 us -> none  [row_squares(): return lax.psum(jnp.sum(total * total, axis=1), 'col')]
    all_gather x0 -> x1, blocking collectives: none -> 14.4 us  [summed_here(): parts = lax.all_gather(x, axis, axis=0, tiled=False)]
    unnamed x14 -> x24, local copies, waits for them, and re-layouts: 7.26 us -> 7.28 us
  transfers between devices with their start and end apart: 1 -> 1, of which waited for: 1 -> 1; matrix products, arithmetic and copies ran while one was open for 5% -> 6% of each run, Pallas kernels for 0% -> 0%
where the time goes in v1:
time: 138 us; the launch traced here: 137 us
  waiting for transfers between devices  47.5 us (34%)
  local copies, waits for them, and re-layouts  37.6 us (27%)
  other arithmetic  23.3 us (17%)
  blocking collectives  14.4 us (10%)
  between operations  14.4 us (10%)
    reduce_scatter x1, waiting for transfers between devices, body(): lax.psum_scatter(jnp.stack(arranged), 'rep', scatter_dimension=2, tiled=T...  47.4 us
    all_gather x1, blocking collectives, summed_here(): parts = lax.all_gather(x, axis, axis=0, tiled=False)  14.4 us
    unnamed x24, local copies, waits for them, and re-layouts  7.28 us
    scatter x4, local copies, waits for them, and re-layouts, body(): blocked[table].at[:, target]  6.23 us
    another operation x2, local copies, waits for them, and re-layouts, body(): grouped = own_grad[table].reshape(width, full_blocks, BLOCK)  5.11 us
    sort x2, other arithmetic, body(): order = jnp.argsort(owner, stable=True)  5.07 us
    gather x2, local copies, waits for them, and re-layouts, body(): jnp.take(grouped, order, axis=1).reshape(width, full_blocks * BLOCK)  4.54 us
    another operation x1, other arithmetic, body(): jnp.stack(arranged)  4.45 us
  transfers between devices with their start and end apart: 1, of which 1 were waited for; matrix products, arithmetic and copies ran while one was open for 6% of the time, Pallas kernels for 0%

profile of v1, /device:TPU:0, one launch (start us, length us, event | category | flops | bytes accessed | tf_op | source)
XLA Modules:
  0.0 137.2 jit_solution(9000679372514960082)
XLA Ops:
  7.2 0.8 and_select_fusion.1
  8.7 2.5 %sort.31 = (s32[128]{0:T(128)}, s32[128]{0:T(128)S(1)}) sort(s32[128]{0:T(128)S(1)} %get-tuple-element.32, s32[128]{0:T(128)S(1)} %iota.7), dimensions={0}, to_apply=%region_0.1 | sort | flops 896 | bytes 2048 | tf_op jit(solution)/shard_map/jit(argsort)/sort | solution.py:31
  11.3 1.2 gather_fusion
  12.5 2.5 %sort.32 = (s32[128]{0:T(128)}, s32[128]{0:T(128)S(1)}) sort(s32[128]{0:T(128)S(1)} %get-tuple-element.33, s32[128]{0:T(128)S(1)} %iota.8), dimensions={0}, to_apply=%region_1.0 | sort | flops 896 | bytes 2048 | tf_op jit(solution)/shard_map/jit(argsort)/sort | solution.py:31
  15.1 1.2 gather_fusion.5
  16.3 1.9 %convert_element_type.4 = f32[1,2,32,16384]{3,2,1,0:T(8,128)S(1)} convert(bf16[1,2,32,16384]{3,2,1,0:T(8,128)(2,1)} %param.14) | non-fusion elementwise | flops 1048576 | bytes 6291456 | tf_op jit(solution)/shard_map/convert_element_type | solution.py:21
  18.2 1.6 %slice_bitcast_fusion.1 = (f32[4,8,128,128]{3,1,2,0:T(8,128)S(1)}, f32[4,8,128,128]{3,1,2,0:T(8,128)}) fusion(f32[1,2,32,16384]{3,2,1,0:T(8,128)S(1)} %convert_element_type.4), kind=kLoop, calls=%fused_computation.14 | loop fusion | bytes 8388608
  20.2 2.6 %copy.25 = f32[32,128,128]{2,0,1:T(8,128)} copy(f32[32,128,128]{2,1,0:T(8,128)S(1)} %bitcast.61) | data formatting | bytes 4194304 | tf_op jit(solution)/shard_map/reshape;squeeze | solution.py:32
  22.8 2.3 %gather_fusion.2 = f32[128,32,128]{2,1,0:T(8,128)S(1)} fusion(f32[32,128,128]{2,0,1:T(8,128)} %copy.25, s32[1024]{0:T(1024)S(1)} %pad_clamp_fusion.3), kind=kCustom, calls=%fused_computation.2.clone | custom fusion | bytes 4194816 | tf_op jit(solution)/shard_map/jit(_take)/gather | solution.py:33
  25.3 1.2 copy.26
  26.5 1.5 %stack_reshape.18 = f32[1,32,16384]{2,1,0:T(8,128)} reshape(f32[32,128,128]{2,1,0:T(8,128)S(1)} %copy.26) | data formatting | bytes 4194304 | tf_op jit(solution)/shard_map/stack;reshape | solution.py:38
  28.0 2.0 %copy.38 = f32[4,8,128,128]{3,2,1,0:T(8,128)S(1)} copy(f32[4,8,128,128]{3,1,2,0:T(8,128)} %get-tuple-element.19) | data formatting | bytes 4194304
  30.0 2.5 %copy.27 = f32[32,128,128]{2,0,1:T(8,128)} copy(f32[32,128,128]{2,1,0:T(8,128)S(1)} %bitcast.62) | data formatting | bytes 4194304 | tf_op jit(solution)/shard_map/reshape;squeeze | solution.py:32
  32.5 2.3 %gather_fusion.3 = f32[128,32,128]{2,1,0:T(8,128)S(1)} fusion(f32[32,128,128]{2,0,1:T(8,128)} %copy.27, s32[1024]{0:T(1024)S(1)} %pad_clamp_fusion.1), kind=kCustom, calls=%fused_computation.6.clone | custom fusion | bytes 4194816 | tf_op jit(solution)/shard_map/jit(_take)/gather | solution.py:33
  35.0 1.2 copy.28
  36.3 1.5 %stack_reshape.19 = f32[1,32,16384]{2,1,0:T(8,128)} reshape(f32[32,128,128]{2,1,0:T(8,128)S(1)} %copy.28) | data formatting | bytes 4194304 | tf_op jit(solution)/shard_map/stack;reshape | solution.py:38
  37.8 4.4 %pad_maximum_fusion = f32[2,32,16384]{2,1,0:T(8,128)} fusion(f32[1,32,16384]{2,1,0:T(8,128)} %stack_reshape.19, f32[1,32,16384]{2,1,0:T(8,128)} %stack_reshape.18), kind=kLoop, calls=%fused_computation.12 | loop fusion | flops 1048576 | bytes 8388608 | tf_op jit(solution)/shard_map/stack | solution.py:38
  42.3 1.7 %slice_bitcast_fusion.3 = (f32[4,8,64,128]{3,1,2,0:T(8,128)S(1)}, f32[4,8,64,128]{3,1,2,0:T(8,128)S(1)}) fusion(f32[2,32,8192]{2,1,0:T(8,128)} %param.12), kind=kLoop, calls=%fused_computation.20 | loop fusion | bytes 4194304
  47.6 1.4 %gather_fusion.6 = f32[32,32,128]{2,1,0:T(8,128)} fusion(f32[32,64,128]{2,0,1:T(8,128)S(1)} %copy.34, s32[1024]{0:T(1024)S(1)} %pad_clamp_fusion), kind=kCustom, calls=%fused_computation.5.clone | custom fusion | bytes 1048704 | tf_op jit(solution)/shard_map/jit(_take)/gather | solution.py:52
  50.3 47.4 %reduce-scatter.2.cloned.1.call-done = f32[2,32,4096]{2,1,0:T(8,128)} async-done(((f32[2,32,16384]{2,1,0:T(8,128)}), f32[2,32,4096]{2,1,0:T(8,128)}) %reduce-scatter.2.cloned.1.call-update) | async-done | bytes 1048592 | tf_op jit(solution)/shard_map/reduce_scatter | solution.py:38
  97.8 1.5 %multiply_reduce_fusion = f32[2,4096]{1,0:T(2,128)S(1)} fusion(f32[2,32,4096]{2,1,0:T(8,128)} %reduce-scatter.2.cloned.1.call-done), kind=kLoop, calls=%fused_computation.19 | loop fusion | flops 516096 | bytes 1081344 | tf_op jit(solution)/shard_map/reduce_sum | solution.py:17
  99.2 14.4 %all-gather.1 = f32[8,2,4096]{2,1,0:T(2,128)S(1)} all-gather(f32[1,2,4096]{2,1,0:T(2,128)S(1)} %bitcast.73), channel_id=2, replica_groups=mesh['rep'=4,'col'=8] {'col'}, dimensions={0}, use_global_device_ids=true | all-gather | bytes 294912 | tf_op jit(solution)/shard_map/all_gather | solution.py:11
  113.6 0.9 fusion.1
  114.7 0.8 slice_multiply_fusion.3
  115.5 0.9 scatter_custom_fusion.2
  116.5 1.8 %fusion.3 = f32[32,32,128]{2,1,0:T(8,128)} fusion(f32[32,32,128]{2,1,0:T(8,128)S(1)} %bitcast.65, f32[32,32,128]{2,1,0:T(8,128)S(1)} %gather_fusion.1, f32[32,128]{1,0:T(8,128)S(1)} %bitcast.75, pred[32]{0:T(512)(128)(4,1)} %copy-done.6), kind=kLoop, calls=%fused_computation.28 | loop fusion | flops 393216 | bytes 1589280 | tf_op jit(solution)/shard_map/sub | solution.py:55
  118.3 3.5 %scatter_fusion = f32[32,64,128]{2,0,1:T(8,128)S(1)} fusion(f32[32,64,128]{2,0,1:T(8,128)S(1)} %copy.30, s32[32]{0:T(128)} %get-tuple-element.35, f32[32,32,128]{2,1,0:T(8,128)} %fusion.3), kind=kCustom, calls=%fused_computation.8 | custom fusion | bytes 1572992 | tf_op jit(solution)/shard_map/scatter | solution.py:57
  122.4 1.2 stack_reshape.20
  123.6 1.1 copy.41
  124.7 0.8 scatter_custom_fusion.3
  125.9 1.5 %scatter_fusion.1 = f32[32,64,128]{2,0,1:T(8,128)S(1)} fusion(f32[32,64,128]{2,0,1:T(8,128)S(1)} %copy.34, s32[32]{0:T(128)S(1)} %copy-done.7, f32[32,32,128]{2,1,0:T(8,128)S(1)} %fusion.2), kind=kCustom, calls=%fused_computation.9 | custom fusion | bytes 1572992 | tf_op jit(solution)/shard_map/scatter | solution.py:57
  128.9 1.5 %pad_maximum_fusion.1 = f32[2,32,8192]{2,1,0:T(8,128)} fusion(f32[1,32,8192]{2,1,0:T(8,128)S(1)} %stack_reshape.21, f32[1,32,8192]{2,1,0:T(8,128)S(1)} %copy-done.1), kind=kLoop, calls=%fused_computation.15 | loop fusion | flops 524288 | bytes 4194304 | tf_op jit(solution)/shard_map/stack | solution.py:62
  (51 shorter events, 9.2 us)
Async XLA Ops:
  7.2 90.6 %reduce-scatter.2.cloned.1.call-start = ((), (), s32[]{:S(2)}) async-start(), calls=%async_computation.1 | async-start | bytes 5242880 | tf_op jit(solution)/shard_map/reduce_scatter | solution.py:38
  44.0 0.9 copy-start.3
  44.9 4.7 %copy-start.4 = (pred[32]{0:T(512)(128)(4,1)}, pred[32]{0:T(512)(128)(4,1)S(1)}, u32[]{:S(2)}) copy-start(pred[32]{0:T(512)(128)(4,1)S(1)} %get-tuple-element.14) | copy-start | bytes 100
  44.9 4.7 %copy-start.6 = (pred[32]{0:T(512)(128)(4,1)}, pred[32]{0:T(512)(128)(4,1)S(1)}, u32[]{:S(2)}) copy-start(pred[32]{0:T(512)(128)(4,1)S(1)} %get-tuple-element.36) | copy-start | bytes 100
  97.7 15.9 %copy-start = (f32[2,32,4096]{2,1,0:T(8,128)S(1)}, f32[2,32,4096]{2,1,0:T(8,128)}, u32[]{:S(2)}) copy-start(f32[2,32,4096]{2,1,0:T(8,128)} %reduce-scatter.2.cloned.1.call-done) | copy-start | bytes 3145732
  122.4 2.3 %copy-start.5 = (pred[32]{0:T(512)(128)(4,1)S(1)}, pred[32]{0:T(512)(128)(4,1)}, u32[]{:S(2)}) copy-start(pred[32]{0:T(512)(128)(4,1)} %copy-done.4) | copy-start | bytes 100
  122.4 2.3 %copy-start.7 = (s32[32]{0:T(128)S(1)}, s32[32]{0:T(128)}, u32[]{:S(2)}) copy-start(s32[32]{0:T(128)} %get-tuple-element.34) | copy-start | bytes 388
  122.4 3.1 %copy-start.2 = (f32[32,32,128]{2,1,0:T(8,128)S(1)}, f32[32,32,128]{2,1,0:T(8,128)}, u32[]{:S(2)}) copy-start(f32[32,32,128]{2,1,0:T(8,128)} %gather_fusion.6) | copy-start | bytes 1572868
  127.4 1.5 %copy-start.1 = (f32[1,32,8192]{2,1,0:T(8,128)S(1)}, f32[1,32,8192]{2,1,0:T(8,128)}, u32[]{:S(2)}) copy-start(f32[1,32,8192]{2,1,0:T(8,128)} %stack_reshape.20) | copy-start | bytes 3145732
Sparse Core Ops, SparseCore 0:
  42.4 55.3 reduce-scatter.1
